TPU v7x, 1024 devices: a whole 8x8x8 slice. The times are simulated.
1024 devices in a mesh: grid: 32 (over z, x_hi), band: 32 (over y, x_lo, core).
Axes of the slice: x: 8 (x_hi: 4, x_lo: 2; x = x_hi * 2 + x_lo), y: 8, z: 8, core: 2. Of those that a mesh axis runs over, the one named last changes fastest.
Arguments:
- psi: bfloat16 [2048, 64, 512], P('band', 'grid'), may hold values from -6 to 6
- ritz_matrix: float32 [2048, 2048], P('band'), may hold values from -0.125 to 0.125
- potential: float32 [64, 512], P('grid'), may hold values from 0.5 to 10, as said below
Outputs:
- rotated: bfloat16 [2048, 64, 512], P('band', 'grid')
- search: bfloat16 [2048, 64, 512], P('band', 'grid')
Inputs may be any that keep to these rules, and one draw needn't show every extreme that they name: `potential`: positive everywhere.
All inputs are finite; a program needn't handle non-finite values.
Results may differ from a plain program's by a relative error of at most 0.0049.
Values may be sent and summed in bfloat16 or wider, within the bound.
A program may use at most 32 MiB of HBM per device.

v0:
```python
import jax
import jax.numpy as jnp
from jax import lax
from jax.sharding import PartitionSpec as P

NZ = 64


epsilon_mean = 1e-06


def with_halo(value, sides, width):
    for axis, dim in sides:
        count, length = (lax.axis_size(axis), value.shape[dim])
        up = [(i, (i + 1) % count) for i in range(count)]
        down = [(j, i) for i, j in up]
        last = lax.slice_in_dim(value, length - width, length, axis=dim)
        first = lax.slice_in_dim(value, 0, width, axis=dim)
        before = lax.ppermute(last, axis, up)
        after = lax.ppermute(first, axis, down)
        value = jnp.concatenate([before, value, after], axis=dim)
    return value


def copy_for_each(value, axis):
    copies = jnp.broadcast_to(value, (lax.axis_size(axis), *value.shape))
    return lax.all_to_all(copies, axis, split_axis=0, concat_axis=0, tiled=True)


def taken_together(value, axis):
    everything = copy_for_each(value, axis)
    return jnp.sum(everything, axis=0)


def in_one(arrays, axis):
    ravelled, at, finished = (jnp.concatenate([a.reshape(-1) for a in arrays]), 0, [])
    so_far = taken_together(ravelled, axis)
    for a in arrays:
        finished.append(so_far[at : at + a.size].reshape(a.shape))
        at += a.size
    return tuple(finished)


def apply_residual(padded, potential):
    center = padded[:, 1:-1].astype(jnp.float32)
    neighbours = padded[:, 2:].astype(jnp.float32) + padded[:, :-2].astype(jnp.float32)
    shaped = center.reshape(center.shape[0], center.shape[1], -1, NZ)
    across = (
        jnp.roll(shaped, 1, 2)
        + jnp.roll(shaped, -1, 2)
        + jnp.roll(shaped, 1, 3)
        + jnp.roll(shaped, -1, 3)
    )
    laplacian = neighbours + across.reshape(center.shape) - 6.0 * center
    resid = -0.5 * laplacian + potential[None] * center
    return (center, resid)


def shards(psi, ritz_matrix, potential):
    band_count = psi.shape[0]
    planes_dev = psi.shape[1]
    face_cells = psi.shape[2]
    piece = lax.all_gather(psi, "band", axis=0, tiled=True)
    flattened = piece.reshape(piece.shape[0], -1).astype(jnp.float32)
    folded = jnp.dot(ritz_matrix, flattened, precision=lax.Precision.HIGHEST)
    rotated = folded.reshape(band_count, planes_dev, face_cells).astype(jnp.bfloat16)
    padded = with_halo(rotated, (("grid", 1),), 1)
    center, resid = apply_residual(padded, potential)
    total_cells = planes_dev * face_cells * lax.axis_size("grid")
    cross_local = jnp.sum(center * resid, axis=(1, 2))
    self_local = jnp.sum(center * center, axis=(1, 2))
    resid_local = jnp.sum(resid * resid, axis=(1, 2))
    cross_sum, self_sum, resid_sum = in_one((cross_local, self_local, resid_local), "grid")
    m_cross = cross_sum / total_cells
    m_plain = self_sum / total_cells
    ratio = m_cross / (m_plain + epsilon_mean)
    direction = resid - ratio[:, None, None] * center
    m_dir = resid_sum / total_cells - 2.0 * ratio * m_cross + ratio * ratio * m_plain
    search = direction * lax.rsqrt(m_dir + epsilon_mean)[:, None, None]
    return (rotated, search.astype(jnp.bfloat16))


def solution(mesh):
    return jax.shard_map(
        shards,
        mesh=mesh,
        in_specs=(P("band", "grid", None), P("band", None), P("grid", None)),
        out_specs=(P("band", "grid", None), P("band", "grid", None)),
        check_vma=False,
    )
```

profile of v0, /device:TPU:1, one launch (start us, length us, event | category | flops | bytes accessed | tf_op | source)
XLA Modules:
  0.0 156.0 jit_solution(10765510547473278407)
XLA Ops:
  7.2 0.0 copy-start
  7.2 0.0 all-gather.2.cloned.1.call-start
  7.2 0.7 all-gather.2.cloned.1.call-update
  7.9 87.3 %all-gather.2.cloned.1.call-done = bf16[2048,2,512]{2,1,0:T(2,128)(2,1)} async-done(((bf16[64,2,512]{2,1,0:T(2,128)(2,1)}), bf16[2048,2,512]{2,1,0:T(2,128)(2,1)}) %all-gather.2.cloned.1.call-update) | async-done | bytes 4194320 | tf_op jit(solution)/shard_map/all_gather | solution.py:63
  95.2 11.2 %copy.18 = bf16[2048,2,512]{0,2,1:T(8,128)(2,1)} copy(bf16[2048,2,512]{2,1,0:T(2,128)(2,1)} %all-gather.2.cloned.1.call-done) | data formatting | bytes 8388608 | tf_op jit(solution)/shard_map/reshape | solution.py:64
  106.4 0.0 copy-done
  106.4 6.1 %fusion.2 = bf16[64,2,512]{2,0,1:T(8,128)(2,1)S(1)} fusion(bf16[2048,2,512]{0,2,1:T(8,128)(2,1)} %copy.18, f32[64,2048]{1,0:T(8,128)S(1)} %copy-done), kind=kOutput, calls=%fused_computation.2 | convolution fusion | flops 1610678272 | bytes 4849664 | tf_op jit(solution)/shard_map/dot_general | solution.py:65
  112.5 0.1 reshape.28
  112.7 0.1 fusion.19
  112.8 0.1 fusion.18
  112.8 0.0 copy-start.1
  112.8 0.2 fusion.17
  113.0 0.2 fusion.16
  113.3 9.6 %collective-permute-start = (bf16[64,1,512]{2,0,1:T(8,128)(2,1)S(1)}, bf16[64,1,512]{2,0,1:T(8,128)(2,1)S(1)}, u32[]{:S(2)}, u32[]{:S(2)}) collective-permute-start(bf16[64,1,512]{2,0,1:T(8,128)(2,1)S(1)} %get-tuple-element.23), channel_id=1, source_target_pairs={{32,0},{64,32},{96,64},{128,96},{160,128},{192,160},{224,192},{256... | collective-permute-start | bytes 196616 | tf_op jit(solution)/shard_map/ppermute | solution.py:20
  122.9 1.9 %collective-permute-start.1 = (bf16[64,1,512]{2,0,1:T(8,128)(2,1)S(1)}, bf16[64,1,512]{2,0,1:T(8,128)(2,1)S(1)}, u32[]{:S(2)}, u32[]{:S(2)}) collective-permute-start(bf16[64,1,512]{2,0,1:T(8,128)(2,1)S(1)} %get-tuple-element.24), channel_id=1, source_target_pairs={{0,32},{32,64},{64,96},{96,128},{128,160},{160,192},{192,224},{224... | collective-permute-start | bytes 196616 | tf_op jit(solution)/shard_map/ppermute | solution.py:19
  124.8 0.5 fusion.6
  125.3 0.1 add.39
  125.4 0.2 collective-permute-done
  125.6 6.6 %collective-permute-done.1 = bf16[64,1,512]{2,0,1:T(8,128)(2,1)S(1)} collective-permute-done((bf16[64,1,512]{2,0,1:T(8,128)(2,1)S(1)}, bf16[64,1,512]{2,0,1:T(8,128)(2,1)S(1)}, u32[]{:S(2)}, u32[]{:S(2)}) %collective-permute-start.1) | collective-permute-done | bytes 65568 | tf_op jit(solution)/shard_map/ppermute | solution.py:19
  132.2 0.0 copy-done.1
  132.2 0.2 fusion.11
  132.5 0.1 pad_maximum_fusion.2
  132.5 0.6 broadcast_in_dim.2
  133.2 3.9 %all-to-all-start = ((f32[32,1,192]{2,1,0:T(1,128)}), f32[32,1,192]{2,1,0:T(1,128)S(1)}, u32[]{:S(2)}, u32[]{:S(2)}) async-start(f32[32,1,192]{2,1,0:T(1,128)} %broadcast_in_dim.2), calls=%async_computation | async-start | bytes 65536 | tf_op jit(solution)/shard_map/all_to_all | solution.py:27
  137.0 0.8 copy.16
  137.8 10.3 %all-to-all-done = f32[32,1,192]{2,1,0:T(1,128)S(1)} async-done(((f32[32,1,192]{2,1,0:T(1,128)}), f32[32,1,192]{2,1,0:T(1,128)S(1)}, u32[]{:S(2)}, u32[]{:S(2)}) %all-to-all-start) | async-done | bytes 24608 | tf_op jit(solution)/shard_map/all_to_all | solution.py:27
  148.1 0.1 reduce_sum.39
  148.1 0.1 add_rsqrt_fusion
  148.2 0.1 fusion.15
  148.4 0.8 copy.17
  (1 shorter events, 0.0 us)
Async XLA Ops:
  7.2 99.2 %copy-start = (f32[64,2048]{1,0:T(8,128)S(1)}, f32[64,2048]{1,0:T(8,128)}, u32[]{:S(2)}) copy-start(f32[64,2048]{1,0:T(8,128)} %param.4) | copy-start | bytes 1572868
  7.2 88.1 %all-gather.2.cloned.1.call-start = ((), (), s32[]{:S(2)}) async-start(), calls=%async_computation.1 | async-start | bytes 4325376 | tf_op jit(solution)/shard_map/all_gather | solution.py:63
  112.8 19.4 %copy-start.1 = (f32[2,512]{1,0:T(2,128)S(1)}, f32[2,512]{1,0:T(2,128)}, u32[]{:S(2)}) copy-start(f32[2,512]{1,0:T(2,128)} %param.5) | copy-start | bytes 12292
  113.3 12.3 %collective-permute-start = (bf16[64,1,512]{2,0,1:T(8,128)(2,1)S(1)}, bf16[64,1,512]{2,0,1:T(8,128)(2,1)S(1)}, u32[]{:S(2)}, u32[]{:S(2)}) collective-permute-start(bf16[64,1,512]{2,0,1:T(8,128)(2,1)S(1)} %get-tuple-element.23), channel_id=1, source_target_pairs={{32,0},{64,32},{96,64},{128,96},{160,128},{192,160},{224,192},{256... | collective-permute-start | bytes 196616 | tf_op jit(solution)/shard_map/ppermute | solution.py:20
  122.9 9.3 %collective-permute-start.1 = (bf16[64,1,512]{2,0,1:T(8,128)(2,1)S(1)}, bf16[64,1,512]{2,0,1:T(8,128)(2,1)S(1)}, u32[]{:S(2)}, u32[]{:S(2)}) collective-permute-start(bf16[64,1,512]{2,0,1:T(8,128)(2,1)S(1)} %get-tuple-element.24), channel_id=1, source_target_pairs={{0,32},{32,64},{64,96},{96,128},{128,160},{160,192},{192,224},{224... | collective-permute-start | bytes 196616 | tf_op jit(solution)/shard_map/ppermute | solution.py:19
  133.2 14.9 %all-to-all-start = ((f32[32,1,192]{2,1,0:T(1,128)}), f32[32,1,192]{2,1,0:T(1,128)S(1)}, u32[]{:S(2)}, u32[]{:S(2)}) async-start(f32[32,1,192]{2,1,0:T(1,128)} %broadcast_in_dim.2), calls=%async_computation | async-start | bytes 65536 | tf_op jit(solution)/shard_map/all_to_all | solution.py:27
Sparse Core Ops, SparseCore 0:
  10.7 84.4 all-gather.1
where the time goes:
time: 158 us; the launch traced here: 156 us
  waiting for transfers between devices  105 us (66%)
  starting transfers between devices  15.4 us (10%)
  local copies, waits for them, and re-layouts  14.3 us (9%)
  between operations  14.1 us (9%)
  matrix products  6.1 us (4%)
    all_gather x1, waiting for transfers between devices, shards(): piece = lax.all_gather(psi, 'band', axis=0, tiled=True)  87.3 us
    reshape x1, local copies, waits for them, and re-layouts, shards(): flattened = piece.reshape(piece.shape[0], -1).astype(jnp.float32)  11.2 us
    all_to_all x1, waiting for transfers between devices, copy_for_each(): return lax.all_to_all(copies, axis, split_axis=0, concat_axis=0, tiled=True)  10.3 us
    ppermute x1, starting transfers between devices, with_halo(): after = lax.ppermute(first, axis, down)  9.63 us
    ppermute x1, waiting for transfers between devices, with_halo(): before = lax.ppermute(last, axis, up)  6.65 us
    dot_general x1, matrix products, shards(): folded = jnp.dot(ritz_matrix, flattened, precision=lax.Precision.HIGHEST)  6.1 us
    all_to_all x1, starting transfers between devices, copy_for_each(): return lax.all_to_all(copies, axis, split_axis=0, concat_axis=0, tiled=True)  3.85 us
  transfers between devices with their start and end apart: 4, of which 4 were waited for; matrix products, arithmetic and copies ran while one was open for 1% of the time, Pallas kernels for 0%

commit v1 on v0

v1 whole, which is shorter than its diff:
```python
import jax
import jax.numpy as jnp
from jax import lax
from jax.experimental import pallas as pl
from jax.experimental.pallas import tpu as pltpu
from jax.sharding import PartitionSpec as P

MESH = pl.DeviceIdType.MESH
F32 = jnp.float32
BF16 = jnp.bfloat16

ZS = 8
XHS = 4
YS = 8
GRID = ZS * XHS
ROWS = 64
CELLS = 512
HALF = CELLS // 2
QUAD = 4 * ROWS
BANDS = YS * QUAD
EPS = 1e-06
TOTAL = 64 * CELLS
LANES = 128


def kernel(
    psi_ref, ritz_ref, pot_ref, rot_ref, search_ref,
    gath, lhs, acc, rv, planes, other, resid, st1, st2,
    ritz_sem, ring_send, ring_recv, sib_send, sib_recv, x_send, x_recv,
    r_send, r_recv, halo_send, halo_recv, s1_send, s1_recv, s2_send, s2_recv,
):
    g = lax.axis_index("grid")
    b = lax.axis_index("band")
    z, xh = lax.div(g, XHS), lax.rem(g, XHS)
    y, xl, c = lax.div(b, 4), lax.rem(lax.div(b, 2), 2), lax.rem(b, 2)

    def band_of(y_, xl_, c_):
        return (y_ * 2 + xl_) * 2 + c_

    def grid_of(z_, xh_):
        return z_ * XHS + xh_

    up = (g, band_of(lax.rem(y + 1, YS), xl, c))
    down = (g, band_of(lax.rem(y + YS - 1, YS), xl, c))
    sib = (g, band_of(y, xl, 1 - c))
    partner = (g, band_of(y, 1 - xl, c))
    outer = (grid_of(z, lax.rem(xh + 2 * xl - 1 + XHS, XHS)), band_of(y, 1 - xl, c))
    g_to = lax.rem(g + 2 * xl - 1 + GRID, GRID)
    g_from = lax.rem(g + 1 - 2 * xl + GRID, GRID)
    halo_own = (g_to, b)
    halo_back = (g_from, b)
    halo_cross = (g_to, band_of(y, 1 - xl, c))
    x_peers = [(grid_of(z, lax.rem(xh + i, XHS)), b) for i in range(1, XHS)]
    z_peers = [(grid_of(lax.rem(z + i, ZS), xh), b) for i in range(1, ZS)]

    ritz_copy = pltpu.make_async_copy(ritz_ref, rv.at[xl], ritz_sem)
    ritz_copy.start()

    barrier = pltpu.get_barrier_semaphore()
    greeted = [up, down, sib, partner, outer, halo_own, halo_back, halo_cross] + x_peers + z_peers
    for device in greeted:
        pl.semaphore_signal(barrier, inc=1, device_id=device, device_id_type=MESH)
    pl.semaphore_wait(barrier, len(greeted))

    sent = []

    def copy_of(src, dst, send_sem, recv_sem, device):
        return pltpu.make_async_remote_copy(
            src_ref=src, dst_ref=dst, send_sem=send_sem, recv_sem=recv_sem,
            device_id=device, device_id_type=MESH,
        )

    def send(*args):
        copy = copy_of(*args)
        copy.start()
        sent.append(copy)

    def arrived(ref, send_sem, recv_sem):
        copy_of(ref, ref, send_sem, recv_sem, sib).wait_recv()

    row = [pl.multiple_of((xl * 2 + c) * ROWS, ROWS), pl.multiple_of(((1 - xl) * 2 + c) * ROWS, ROWS)]
    sib_row = [
        pl.multiple_of((xl * 2 + 1 - c) * ROWS, ROWS),
        pl.multiple_of(((1 - xl) * 2 + 1 - c) * ROWS, ROWS),
    ]

    def cells(q):
        return pl.ds(q * HALF, HALF)

    def chunk(rel, kind, q):
        return gath.at[rel, pl.ds(row[kind], ROWS), cells(q)]

    def sib_chunk(rel, kind, q):
        return gath.at[rel, pl.ds(sib_row[kind], ROWS), cells(q)]

    def to_up(src, rel, kind, q):
        send(src, chunk(rel + 1, kind, q), ring_send.at[0, rel, kind, q], ring_recv.at[rel + 1, kind, q], up)

    def to_down(src, rel, kind, q):
        to = (rel + YS - 1) % YS
        send(src, chunk(to, kind, q), ring_send.at[1, (YS - rel) % YS, kind, q], ring_recv.at[to, kind, q], down)

    def to_sib(src, rel, kind, q):
        send(src, chunk(rel, kind, q), sib_send.at[rel, kind, q], sib_recv.at[rel, kind, q], sib)

    def ring_arrived(rel, kind, q):
        arrived(chunk(rel, kind, q), sib_send.at[rel, kind, q], ring_recv.at[rel, kind, q])

    def sib_arrived(rel, kind, q):
        arrived(sib_chunk(rel, kind, q), sib_send.at[rel, kind, q], sib_recv.at[rel, kind, q])

    for q in range(2):
        send(psi_ref.at[1 - xl, :, cells(q)], chunk(0, 0, q), x_send.at[q], x_recv.at[q], partner)
    for q in range(2):
        src = psi_ref.at[xl, :, cells(q)]
        to_up(src, 0, 0, q)
        to_down(src, 0, 0, q)
        to_sib(src, 0, 0, q)

    ritz_copy.wait()
    part = ROWS // 2
    send(rv.at[xl, pl.ds(0, part)], rv.at[xl, pl.ds(0, part)], r_send.at[0], r_recv.at[0], partner)
    send(rv.at[xl, pl.ds(part, part)], rv.at[xl, pl.ds(part, part)], r_send.at[1], r_recv.at[1], outer)

    gath[0, pl.ds(row[0], ROWS), :] = psi_ref[xl]

    def split_ritz(who):
        hi_at = pl.ds(pl.multiple_of(who * ROWS, ROWS), ROWS)
        lo_at = pl.ds(pl.multiple_of(2 * ROWS + who * ROWS, ROWS), ROWS)
        for yy in range(YS):
            value = rv[who, :, yy * QUAD : (yy + 1) * QUAD]
            high = value.astype(BF16)
            lhs[yy, hi_at, :] = high
            lhs[yy, lo_at, :] = (value - high.astype(F32)).astype(BF16)

    split_ritz(xl)

    for q in range(2):
        arrived(chunk(0, 1, q), x_send.at[q], x_recv.at[q])
        src = chunk(0, 1, q)
        to_up(src, 0, 1, q)
        to_down(src, 0, 1, q)
        to_sib(src, 0, 1, q)

    first = [True, True]

    def multiply(rel, q):
        for kind in range(2):
            sib_arrived(rel, kind, q)
        owner = lax.rem(y - rel + YS, YS)
        term = jnp.dot(lhs[owner], gath[rel, :, q * HALF : (q + 1) * HALF], preferred_element_type=F32)
        if first[q]:
            acc[q] = term
            first[q] = False
        else:
            acc[q] += term

    def handle(d, kind, q):
        rel = d
        ring_arrived(rel, kind, q)
        if d < 3 or kind == 0:
            to_up(chunk(rel, kind, q), rel, kind, q)
        to_sib(chunk(rel, kind, q), rel, kind, q)
        rel = YS - d
        ring_arrived(rel, kind, q)
        if d < 3 or kind == 1:
            to_down(chunk(rel, kind, q), rel, kind, q)
        to_sib(chunk(rel, kind, q), rel, kind, q)

    for d in (1, 2):
        for kind in range(2):
            for q in range(2):
                handle(d, kind, q)

    handle(3, 0, 0)
    arrived(rv.at[1 - xl, pl.ds(0, part)], r_send.at[0], r_recv.at[0])
    arrived(rv.at[1 - xl, pl.ds(part, part)], r_send.at[1], r_recv.at[1])
    split_ritz(1 - xl)
    handle(3, 0, 1)
    for rel in (0, 1):
        for q in range(2):
            multiply(rel, q)
    handle(3, 1, 0)
    for rel in (7, 2):
        for q in range(2):
            multiply(rel, q)
    handle(3, 1, 1)
    for q in range(2):
        multiply(6, q)
    for rel in (3, 5):
        for q in range(2):
            multiply(rel, q)

    slot = 3 * (1 - xl)
    for q in range(2):
        at = slice(q * HALF, (q + 1) * HALF)
        for kind in range(2):
            ring_arrived(4, kind, q)
            to_sib(chunk(4, kind, q), 4, kind, q)
        multiply(4, q)

        def rows_of(who):
            high = acc[q, pl.ds(pl.multiple_of(who * ROWS, ROWS), ROWS), :]
            low = acc[q, pl.ds(pl.multiple_of(2 * ROWS + who * ROWS, ROWS), ROWS), :]
            return (high + low).astype(BF16)

        other[:, at] = rows_of(1 - xl)
        planes[1 + xl, :, at] = rows_of(xl)
        src = other.at[:, cells(q)]
        send(src, planes.at[1 + xl, :, cells(q)], halo_send.at[0, q], halo_recv.at[1 + xl, q], partner)
        send(src, planes.at[slot, :, cells(q)], halo_send.at[1, q], halo_recv.at[slot, q], halo_cross)
        src = planes.at[1 + xl, :, cells(q)]
        send(src, planes.at[slot, :, cells(q)], halo_send.at[2, q], halo_recv.at[slot, q], halo_own)

    for q in range(2):
        for at in (0, 2 - xl, 3):
            arrived(planes.at[at, :, cells(q)], halo_send.at[0, q], halo_recv.at[at, q])

    lane = lax.broadcasted_iota(jnp.int32, (ROWS, LANES), 1)
    low_half = lane < 64
    z_last = lax.rem(lane, 64) == 63
    z_first = lax.rem(lane, 64) == 0
    tiles = CELLS // LANES
    sums = [None, None, None]
    for p in range(2):
        center = [planes[1 + p, :, t * LANES : (t + 1) * LANES].astype(F32) for t in range(tiles)]
        turned = [pltpu.roll(v, 64, 1) for v in center]
        for t in range(tiles):
            at = slice(t * LANES, (t + 1) * LANES)
            v = center[t]
            below = planes[p, :, at].astype(F32)
            above = planes[p + 2, :, at].astype(F32)
            across_y = turned[t] + jnp.where(low_half, turned[(t + tiles - 1) % tiles], turned[(t + 1) % tiles])
            after = jnp.where(z_last, pltpu.roll(v, 63, 1), pltpu.roll(v, LANES - 1, 1))
            before = jnp.where(z_first, pltpu.roll(v, LANES - 63, 1), pltpu.roll(v, 1, 1))
            laplacian = (below + above) + across_y + (after + before) - 6.0 * v
            value = -0.5 * laplacian + pot_ref[p : p + 1, at] * v
            resid[p, :, at] = value
            for i, term in enumerate((v * value, v * v, value * value)):
                sums[i] = term if sums[i] is None else sums[i] + term
        rot_ref[p] = planes[1 + p]

    cols = [jnp.sum(s, axis=1, keepdims=True) for s in sums]
    packed = jnp.where(lane == 0, cols[0], jnp.where(lane == 1, cols[1], jnp.where(lane == 2, cols[2], 0.0)))
    square = jnp.concatenate([packed, jnp.zeros((LANES - ROWS, LANES), F32)], axis=0)
    st1[0] = jnp.transpose(square)[0:8]
    for i, device in enumerate(x_peers, 1):
        send(st1.at[0], st1.at[i], s1_send.at[i], s1_recv.at[i], device)
    for i in range(1, XHS):
        arrived(st1.at[i], s1_send.at[i], s1_recv.at[i])
    st2[0] = (st1[0] + st1[1]) + (st1[2] + st1[3])
    for i, device in enumerate(z_peers, 1):
        send(st2.at[0], st2.at[i], s2_send.at[i], s2_recv.at[i], device)
    total = st2[0]
    for i in range(1, ZS):
        arrived(st2.at[i], s2_send.at[i], s2_recv.at[i])
        total = total + st2[i]
    total = total / TOTAL
    m_cross, m_plain, m_resid = total[0:1], total[1:2], total[2:3]
    ratio = m_cross / (m_plain + EPS)
    m_dir = m_resid - 2.0 * ratio * m_cross + ratio * ratio * m_plain
    scale = lax.rsqrt(m_dir + EPS)
    line = lax.broadcasted_iota(jnp.int32, (LANES, LANES), 0)
    both = jnp.transpose(jnp.where(line == 0, ratio, jnp.where(line == 1, scale, 0.0)))
    ratio_col, scale_col = both[0:ROWS, 0:1], both[0:ROWS, 1:2]
    for p in range(2):
        for t in range(tiles):
            at = slice(t * LANES, (t + 1) * LANES)
            v = planes[1 + p, :, at].astype(F32)
            search_ref[p, :, at] = ((resid[p, :, at] - ratio_col * v) * scale_col).astype(BF16)

    for copy in sent:
        copy.wait_send()


def shards(psi, ritz_matrix, potential):
    dma = pltpu.SemaphoreType.DMA
    vmem = pl.BlockSpec(memory_space=pltpu.VMEM)
    shape = jax.ShapeDtypeStruct((2, ROWS, CELLS), BF16)
    rotated, search = pl.pallas_call(
        kernel,
        out_shape=(shape, shape),
        in_specs=[vmem, pl.BlockSpec(memory_space=pltpu.HBM), vmem],
        out_specs=(vmem, vmem),
        scratch_shapes=[
            pltpu.VMEM((YS, QUAD, CELLS), BF16),
            pltpu.VMEM((YS, QUAD, QUAD), BF16),
            pltpu.VMEM((2, QUAD, HALF), F32),
            pltpu.VMEM((2, ROWS, BANDS), F32),
            pltpu.VMEM((4, ROWS, CELLS), BF16),
            pltpu.VMEM((ROWS, CELLS), BF16),
            pltpu.VMEM((2, ROWS, CELLS), F32),
            pltpu.VMEM((XHS, 8, LANES), F32),
            pltpu.VMEM((ZS, 8, LANES), F32),
            dma(()),
            dma((2, 4, 2, 2)),
            dma((YS, 2, 2)),
            dma((YS, 2, 2)),
            dma((YS, 2, 2)),
            dma((2,)),
            dma((2,)),
            dma((2,)),
            dma((2,)),
            dma((3, 2)),
            dma((4, 2)),
            dma((XHS,)),
            dma((XHS,)),
            dma((ZS,)),
            dma((ZS,)),
        ],
        compiler_params=pltpu.CompilerParams(
            collective_id=0, has_side_effects=True, vmem_limit_bytes=32 * 1024 * 1024
        ),
    )(jnp.transpose(psi, (1, 0, 2)), ritz_matrix, potential)
    return (jnp.transpose(rotated, (1, 0, 2)), jnp.transpose(search, (1, 0, 2)))


def solution(mesh):
    return jax.shard_map(
        shards,
        mesh=mesh,
        in_specs=(P("band", "grid", None), P("band", None), P("grid", None)),
        out_specs=(P("band", "grid", None), P("band", "grid", None)),
        check_vma=False,
    )
```

time: 158 us -> 60.5 us (0.38)
  the two profiles are of different devices: /device:TPU:1 before, /device:TPU:10 now
where the time goes in v1:
time: 60.5 us; the launch traced here: 60.3 us
  Pallas kernels  56.1 us (93%)
  local copies, waits for them, and re-layouts  3.55 us (6%)
  between operations  0.67 us (1%)
    pallas_call x1, Pallas kernels, shards(): pl.pallas_call(kernel, out_shape=(shape, shape), in_specs=[vmem, pl.Block...  56.1 us
    unnamed x7, local copies, waits for them, and re-layouts  3.55 us

profile of v1, /device:TPU:10, one launch (start us, length us, event | category | flops | bytes accessed | tf_op | source)
XLA Modules:
  0.0 60.3 jit_solution(7243410187854984690)
XLA Ops:
  0.6 0.0 copy-start.1
  0.6 0.9 %copy.9 = bf16[64,2,512]{2,0,1:T(8,128)(2,1)S(1)} copy(bf16[64,2,512]{2,1,0:T(2,128)(2,1)} %param.3) | data formatting | bytes 262144 | tf_op args[0]
  1.6 0.0 copy-done.1
  1.6 0.0 copy-start
  1.6 1.0 %copy-done = f32[64,2048]{1,0:T(8,128)S(1)} copy-done((f32[64,2048]{1,0:T(8,128)S(1)}, f32[64,2048]{1,0:T(8,128)}, u32[]{:S(2)}) %copy-start) | copy-done | bytes 524312
  2.6 56.1 %shard_map.50 = (bf16[2,64,512]{2,1,0:T(8,128)(2,1)S(1)}, bf16[2,64,512]{2,1,0:T(8,128)(2,1)S(1)}) custom-call(bf16[2,64,512]{2,1,0:T(8,128)(2,1)S(1)} %bitcast.5, f32[64,2048]{1,0:T(8,128)S(1)} %copy-done, f32[2,512]{1,0:T(2,128)S(1)} %copy-done.1), custom_call_target="tpu_custom_call" | custom-call | tf_op jit(solution)/shard_map/pallas_call | solution.py:280
  58.7 0.8 %copy.6 = bf16[64,2,512]{2,1,0:T(2,128)(2,1)} copy(bf16[64,2,512]{2,0,1:T(8,128)(2,1)S(1)} %bitcast.7) | data formatting | bytes 262144
  59.5 0.8 %copy.7 = bf16[64,2,512]{2,1,0:T(2,128)(2,1)} copy(bf16[64,2,512]{2,0,1:T(8,128)(2,1)S(1)} %bitcast.6) | data formatting | bytes 262144
Async XLA Ops:
  0.6 0.9 %copy-start.1 = (f32[2,512]{1,0:T(2,128)S(1)}, f32[2,512]{1,0:T(2,128)}, u32[]{:S(2)}) copy-start(f32[2,512]{1,0:T(2,128)} %pot_ref.1) | copy-start | bytes 12292
  1.6 1.0 %copy-start = (f32[64,2048]{1,0:T(8,128)S(1)}, f32[64,2048]{1,0:T(8,128)}, u32[]{:S(2)}) copy-start(f32[64,2048]{1,0:T(8,128)} %ritz_ref.1) | copy-start | bytes 1572868
